TPU v7x, 32 devices: a whole 2x2x4 slice. The times are simulated.
32 devices in a mesh: ctx: 8 (over z, y), fsdp: 4 (over x, core).
Axes of the slice: x: 2, y: 2, z: 4, core: 2. Of those that a mesh axis runs over, the one named last changes fastest.
Arguments:
- tokens: bfloat16 [4, 1024, 1600], P('fsdp', 'ctx'), may hold values from -6 to 6
- block_order: int32 [4, 16], P('fsdp'), may hold values from 0 to 15, each once within a row
- qkv_weight: bfloat16 [1600, 4800], P('fsdp'), may hold values from -0.15625 to 0.15625
- query_bias: float32 [1600], replicated, may hold values from -3 to 3
- value_bias: float32 [1600], replicated, may hold values from -0.18 to 0.18
- out_weight: bfloat16 [1600, 1600], P('fsdp'), may hold values from -2.5 to 2.5
- out_bias: float32 [1600], replicated, may hold values from -1.8 to 1.8
- expand_weight: bfloat16 [1600, 6400], P('fsdp'), may hold values from -0.15625 to 0.15625
- expand_bias: float32 [6400], replicated, may hold values from -3 to 3
- shrink_weight: bfloat16 [6400, 1600], P('fsdp'), may hold values from -0.078125 to 0.078125
- shrink_bias: float32 [1600], replicated, may hold values from -1.8 to 1.8
- first_gain: float32 [1600], replicated, may hold values from 0.5 to 1.5
- first_shift: float32 [1600], replicated, may hold values from -1.8 to 1.8
- second_gain: float32 [1600], replicated, may hold values from 0.5 to 1.5
- second_shift: float32 [1600], replicated, may hold values from -1.8 to 1.8
- cotangent: bfloat16 [4, 1024, 1600], P('fsdp', 'ctx'), may hold values from -6 to 6
Outputs:
- result: bfloat16 [4, 1024, 1600], P('fsdp', 'ctx')
- grad_tokens: float32 [4, 1024, 1600], P('fsdp', 'ctx')
- grad_qkv: float32 [1600, 4800], P('fsdp', 'ctx')
- grad_outw: float32 [1600, 1600], P('fsdp', 'ctx')
- grad_expand: float32 [1600, 6400], P('fsdp', 'ctx')
- grad_shrink: float32 [6400, 1600], P('fsdp', 'ctx')
- grad_query_bias: float32 [1600], replicated
- grad_value_bias: float32 [1600], replicated
- grad_out_bias: float32 [1600], replicated
- grad_expand_bias: float32 [6400], replicated
- grad_shrink_bias: float32 [1600], replicated
- grad_first_gain: float32 [1600], replicated
- grad_first_shift: float32 [1600], replicated
- grad_second_gain: float32 [1600], replicated
- grad_second_shift: float32 [1600], replicated
Inputs may be any that keep to these rules, and one draw needn't show every extreme that they name: Each row of block_order names every block of its sequence once.
All inputs are finite; a program needn't handle non-finite values.
Results may differ from a plain program's by a relative error of at most 0.015.
Values may be sent and summed in bfloat16 or wider, within the bound.
A program may use at most 384 MiB of HBM per device.

v0:
```python
import jax
import jax.numpy as jnp
from jax import lax
from jax.sharding import PartitionSpec as P

HEADS = 25
HEAD_DIM = 64
EPSILON = 1e-05


def layer_norm(values, gain, shift):
    center = jnp.mean(values, axis=-1, keepdims=True)
    centred = values - center
    spread = jnp.mean(centred * centred, axis=-1, keepdims=True)
    return centred * lax.rsqrt(spread + EPSILON) * gain + shift


def smooth_gelu(values):
    return (
        0.5
        * values
        * (1.0 + jnp.tanh(0.7978845608028654 * (values + 0.044715 * values * values * values)))
    )


def fetch(weight):
    return lax.all_gather(weight, "fsdp", axis=0, tiled=True)


def against(left, weight):
    return lax.dot_general(
        left, weight, (((1,), (1,)), ((), ())), preferred_element_type=jnp.float32
    )


def shard_rows(local):
    return lax.psum_scatter(
        local.astype(jnp.bfloat16), "fsdp", scatter_dimension=0, tiled=True
    ).astype(jnp.float32)


def column_grad(left, right):
    whole_left = lax.all_gather(left, "ctx", axis=0, tiled=True)
    right_columns = lax.all_to_all(right, "ctx", split_axis=1, concat_axis=0, tiled=True)
    local = lax.dot_general(
        whole_left, right_columns, (((0,), (0,)), ((), ())), preferred_element_type=jnp.float32
    )
    return shard_rows(local)


def shared_grad(left, right):
    return column_grad(left, right)


def masked_scores(queries, query_pos, keys, key_pos, factor):
    scores = jnp.einsum("qhd,khd->hqk", queries, keys, preferred_element_type=jnp.float32) * factor
    allowed = (key_pos[None, :] <= query_pos[:, None])[None]
    return jnp.where(allowed, scores, -jnp.inf)


def body(
    tokens,
    block_order,
    qkv_weight,
    query_bias,
    value_bias,
    out_weight,
    out_bias,
    expand_weight,
    expand_bias,
    shrink_weight,
    shrink_bias,
    first_gain,
    first_shift,
    second_gain,
    second_shift,
    cotangent,
):
    inputs = tokens[0].astype(jnp.float32)
    rows = inputs.shape[0]
    width = inputs.shape[1]
    half = rows // 2
    factor = HEAD_DIM ** (-0.5)
    place = lax.axis_index("ctx")
    key_pos = (block_order[0][:, None] * half + jnp.arange(half, dtype=jnp.int32)[None, :]).reshape(
        -1
    )
    length = key_pos.shape[0]
    query_pos = lax.dynamic_slice_in_dim(key_pos, place * rows, rows)
    block = min(512, length)
    count = length // block
    normed_one = layer_norm(inputs, first_gain, first_shift)
    lowered_one = normed_one.astype(jnp.bfloat16)
    project = jnp.dot(lowered_one, fetch(qkv_weight), preferred_element_type=jnp.float32)
    query = (project[:, :width] + query_bias).astype(jnp.bfloat16)
    keys_own = project[:, width : 2 * width].astype(jnp.bfloat16)
    values_own = (project[:, 2 * width :] + value_bias).astype(jnp.bfloat16)
    all_keys, all_values = (
        lax.all_gather(keys_own, "ctx", axis=0, tiled=True),
        lax.all_gather(values_own, "ctx", axis=0, tiled=True),
    )
    query_heads = query.reshape(rows, HEADS, HEAD_DIM)
    key_blocks = all_keys.reshape(count, block, HEADS, HEAD_DIM)
    value_blocks = all_values.reshape(count, block, HEADS, HEAD_DIM)
    pos_blocks = key_pos.reshape(count, block)

    def running(carry, pieces):
        highest, total = carry
        key_piece, pos_piece = pieces
        scores = masked_scores(query_heads, query_pos, key_piece, pos_piece, factor)
        fresh = jnp.maximum(highest, jnp.max(scores, axis=-1))
        total = total * jnp.exp(highest - fresh) + jnp.sum(
            jnp.exp(scores - fresh[..., None]), axis=-1
        )
        return ((fresh, total), None)

    start = (jnp.full((HEADS, rows), -1e30, jnp.float32), jnp.zeros((HEADS, rows), jnp.float32))
    (highest, total), unused = lax.scan(running, start, (key_blocks, pos_blocks))
    log_sum = highest + jnp.log(total)

    def weighted(acc, pieces):
        key_piece, value_piece, pos_piece = pieces
        scores = masked_scores(query_heads, query_pos, key_piece, pos_piece, factor)
        probs = jnp.exp(scores - log_sum[..., None]).astype(jnp.bfloat16)
        return (
            acc
            + jnp.einsum("hqk,khd->qhd", probs, value_piece, preferred_element_type=jnp.float32),
            None,
        )

    attended_heads, unused = lax.scan(
        weighted,
        jnp.zeros((rows, HEADS, HEAD_DIM), jnp.float32),
        (key_blocks, value_blocks, pos_blocks),
    )
    attended = attended_heads.reshape(rows, width)
    attended_low = attended.astype(jnp.bfloat16)
    middle = (
        inputs
        + jnp.dot(attended_low, fetch(out_weight), preferred_element_type=jnp.float32)
        + out_bias
    )
    normed_two = layer_norm(middle, second_gain, second_shift)
    lowered_two = normed_two.astype(jnp.bfloat16)
    expanded = (
        jnp.dot(lowered_two, fetch(expand_weight), preferred_element_type=jnp.float32) + expand_bias
    )
    hidden_low = smooth_gelu(expanded).astype(jnp.bfloat16)
    shrink_full = fetch(shrink_weight)
    result = (
        middle + jnp.dot(hidden_low, shrink_full, preferred_element_type=jnp.float32) + shrink_bias
    )
    grad_low = cotangent[0]
    grad_result = grad_low.astype(jnp.float32)
    grad_shrink = shared_grad(hidden_low, grad_low)
    grad_shrink_bias = jnp.sum(grad_result, axis=0)
    grad_hidden = against(grad_low, shrink_full)
    unused, gelu_back = jax.vjp(smooth_gelu, expanded)
    (grad_expanded,) = gelu_back(grad_hidden)
    expanded_low = grad_expanded.astype(jnp.bfloat16)
    grad_expand_bias = jnp.sum(expanded_low.astype(jnp.float32), axis=0)
    grad_expand = shared_grad(lowered_two, expanded_low)
    grad_normed_two = against(expanded_low, fetch(expand_weight))
    unused, second_back = jax.vjp(layer_norm, middle, second_gain, second_shift)
    grad_middle_norm, grad_second_gain, grad_second_shift = second_back(grad_normed_two)
    grad_middle = grad_result + grad_middle_norm
    middle_low = grad_middle.astype(jnp.bfloat16)
    grad_out_bias = jnp.sum(middle_low.astype(jnp.float32), axis=0)
    grad_outw = shared_grad(attended_low, middle_low)
    grad_att_low = against(middle_low, fetch(out_weight)).astype(jnp.bfloat16)
    grad_att_heads = grad_att_low.reshape(rows, HEADS, HEAD_DIM)
    delta = jnp.sum(grad_att_heads.astype(jnp.float32) * attended_heads, axis=-1).T

    def key_step(acc, pieces):
        key_piece, value_piece, pos_piece = pieces
        scores = masked_scores(query_heads, query_pos, key_piece, pos_piece, factor)
        probs = jnp.exp(scores - log_sum[..., None])
        slopes = jnp.einsum(
            "qhd,khd->hqk", grad_att_heads, value_piece, preferred_element_type=jnp.float32
        )
        score_grad = (probs * (slopes - delta[..., None])).astype(jnp.bfloat16)
        acc = acc + jnp.einsum(
            "hqk,khd->qhd", score_grad, key_piece, preferred_element_type=jnp.float32
        )
        return (acc, (probs.astype(jnp.bfloat16), score_grad))

    empty_heads = jnp.zeros((rows, HEADS, HEAD_DIM), jnp.float32)

    def query_step(acc, pieces):
        acc, unused_pair = key_step(acc, pieces)
        return (acc, None)

    query_acc, unused = lax.scan(query_step, empty_heads, (key_blocks, value_blocks, pos_blocks))
    all_queries, all_grads = (
        lax.all_gather(query, "ctx", axis=0, tiled=True),
        lax.all_gather(grad_att_low, "ctx", axis=0, tiled=True),
    )
    all_sums, all_deltas = (
        lax.all_gather(log_sum.T, "ctx", axis=0, tiled=True),
        lax.all_gather(delta.T, "ctx", axis=0, tiled=True),
    )
    own_keys = keys_own.reshape(rows, HEADS, HEAD_DIM)
    own_values = values_own.reshape(rows, HEADS, HEAD_DIM)

    def owner_step(carry, pieces):
        key_acc, value_acc = carry
        query_piece, grad_piece, sum_piece, delta_piece, pos_piece = pieces
        scores = masked_scores(query_piece, pos_piece, own_keys, query_pos, factor)
        probs = jnp.exp(scores - sum_piece.T[..., None])
        slopes = jnp.einsum(
            "qhd,khd->hqk", grad_piece, own_values, preferred_element_type=jnp.float32
        )
        score_grad = (probs * (slopes - delta_piece.T[..., None])).astype(jnp.bfloat16)
        key_acc = key_acc + jnp.einsum(
            "hqk,qhd->khd", score_grad, query_piece, preferred_element_type=jnp.float32
        )
        value_acc = value_acc + jnp.einsum(
            "hqk,qhd->khd",
            probs.astype(jnp.bfloat16),
            grad_piece,
            preferred_element_type=jnp.float32,
        )
        return ((key_acc, value_acc), None)

    (key_acc, value_acc), unused = lax.scan(
        owner_step,
        (empty_heads, empty_heads),
        (
            all_queries.reshape(count, block, HEADS, HEAD_DIM),
            all_grads.reshape(count, block, HEADS, HEAD_DIM),
            all_sums.reshape(count, block, HEADS),
            all_deltas.reshape(count, block, HEADS),
            pos_blocks,
        ),
    )
    grad_keys = key_acc.reshape(rows, width)
    grad_values = value_acc.reshape(rows, width)
    grad_query_low = (query_acc.reshape(rows, width) * factor).astype(jnp.bfloat16)
    grad_key_low = (grad_keys * factor).astype(jnp.bfloat16)
    grad_value_low = grad_values.astype(jnp.bfloat16)
    project_grad = jnp.concatenate([grad_query_low, grad_key_low, grad_value_low], axis=1)
    grad_query_bias = jnp.sum(grad_query_low.astype(jnp.float32), axis=0)
    grad_value_bias = jnp.sum(grad_value_low.astype(jnp.float32), axis=0)
    grad_qkv = shared_grad(lowered_one, project_grad)
    grad_normed_one = against(project_grad, fetch(qkv_weight))
    unused, first_back = jax.vjp(layer_norm, inputs, first_gain, first_shift)
    grad_first_input, grad_first_gain, grad_first_shift = first_back(grad_normed_one)
    grad_inputs = grad_middle + grad_first_input
    summed = lax.psum(
        (
            grad_query_bias,
            grad_value_bias,
            grad_out_bias,
            grad_expand_bias,
            grad_shrink_bias,
            grad_first_gain,
            grad_first_shift,
            grad_second_gain,
            grad_second_shift,
        ),
        ("ctx", "fsdp"),
    )
    return (
        result.astype(jnp.bfloat16)[None],
        grad_inputs[None],
        grad_qkv,
        grad_outw,
        grad_expand,
        grad_shrink,
        summed[0],
        summed[1],
        summed[2],
        summed[3],
        summed[4],
        summed[5],
        summed[6],
        summed[7],
        summed[8],
    )


def solution(mesh):
    placed = (
        P("fsdp", "ctx", None),
        P("fsdp", None),
        P("fsdp", None),
        P(),
        P(),
        P("fsdp", None),
        P(),
        P("fsdp", None),
        P(),
        P("fsdp", None),
        P(),
        P(),
        P(),
        P(),
        P(),
        P("fsdp", "ctx", None),
    )
    return jax.shard_map(
        body,
        mesh=mesh,
        in_specs=placed,
        out_specs=(
            P("fsdp", "ctx", None),
            P("fsdp", "ctx", None),
            P("fsdp", "ctx"),
            P("fsdp", "ctx"),
            P("fsdp", "ctx"),
            P("fsdp", "ctx"),
            P(),
            P(),
            P(),
            P(),
            P(),
            P(),
            P(),
            P(),
            P(),
        ),
        check_vma=False,
    )
```

profile of v0, /device:TPU:8, one launch (start us, length us, event | category | flops | bytes accessed | tf_op | source)
XLA Modules:
  0.0 1413.1 jit_solution(10884619457395824276)
XLA Ops:
  9.8 100.0 %all-gather.13.cloned.1.call-done = bf16[1600,4800]{1,0:T(8,128)(2,1)} async-done(((bf16[400,4800]{1,0:T(8,128)(2,1)}), bf16[1600,4800]{1,0:T(8,128)(2,1)}) %all-gather.13.cloned.1.call-update) | async-done | bytes 15360016 | tf_op jit(solution)/shard_map/all_gather | solution.py:27
  125.1 57.6 %all-gather.17.cloned.1.call-done = bf16[1024,1600]{0,1:T(8,128)(2,1)} async-done(((bf16[128,1600]{0,1:T(8,128)(2,1)}), bf16[1024,1600]{0,1:T(8,128)(2,1)}) %all-gather.17.cloned.1.call-update) | async-done | bytes 3276816 | tf_op jit(solution)/shard_map/all_gather | solution.py:99
  193.9 53.8 %all-gather.15.cloned.1.call-done = bf16[1024,1600]{0,1:T(8,128)(2,1)} async-done(((bf16[128,1600]{0,1:T(8,128)(2,1)}), bf16[1024,1600]{0,1:T(8,128)(2,1)}) %all-gather.15.cloned.1.call-update) | async-done | bytes 3276816 | tf_op jit(solution)/shard_map/all_gather | solution.py:100
  261.0 19.3 %while.48 = (s32[]{:T(128)}, f32[25,128]{1,0:T(8,128)S(1)}, f32[25,128]{1,0:T(8,128)S(1)}, s32[2,512]{1,0:T(2,128)S(1)}, s32[128]{0:T(128)S(1)}, /*index=5*/bf16...) while((s32[]{:T(128)}, f32[25,128]{1,0:T(8,128)S(1)}, ...), condition=%wide.region_5.6_spmd.clone, body=%wide.region_2.5_spmd.clone.sunk | while | flops 221265536 | bytes 15524976 | solution.py:118
  280.4 10.0 while.49
  300.1 120.2 %all-gather.21.cloned.1.call-done = bf16[1600,6400]{1,0:T(8,128)(2,1)} async-done(((bf16[400,6400]{1,0:T(8,128)(2,1)}), bf16[1600,6400]{1,0:T(8,128)(2,1)}) %all-gather.21.cloned.1.call-update) | async-done | bytes 20480016 | tf_op jit(solution)/shard_map/all_gather | solution.py:27
  420.3 14.0 multiply_convert_fusion.6
  434.3 120.9 %all-gather.23.cloned.1.call-done = bf16[6400,1600]{1,0:T(8,128)(2,1)} async-done(((bf16[1600,1600]{1,0:T(8,128)(2,1)}), bf16[6400,1600]{1,0:T(8,128)(2,1)}) %all-gather.23.cloned.1.call-update) | async-done | bytes 20480016 | tf_op jit(solution)/shard_map/all_gather | solution.py:27
  555.2 12.3 convert_reduce_fusion
  567.5 12.8 multiply_reduce_fusion
  593.0 42.4 %all_gather.52 = f32[1024,25]{0,1:T(8,128)S(1)} all-gather(f32[128,25]{0,1:T(8,128)S(1)} %bitcast.354), channel_id=1, replica_groups=mesh['ctx'=8,'fsdp'=4] {'ctx'}, dimensions={0}, use_global_device_ids=true | all-gather | bytes 115200 | tf_op jit(solution)/shard_map/all_gather | solution.py:199
  662.5 58.5 %all-gather.31.cloned.1.call-done = bf16[1024,1600]{0,1:T(8,128)(2,1)} async-done(((bf16[128,1600]{0,1:T(8,128)(2,1)}), bf16[1024,1600]{0,1:T(8,128)(2,1)}) %all-gather.31.cloned.1.call-update) | async-done | bytes 3276816 | tf_op jit(solution)/shard_map/all_gather | solution.py:43
  725.0 24.6 %while.50 = (s32[]{:T(128)}, f32[128,25,64]{0,2,1:T(8,128)}, bf16[2,512,25,64]{1,3,2,0:T(8,128)(2,1)S(1)}, s32[2,512]{1,0:T(2,128)S(1)}, s32[128]{0:T(128)S(1)},...) while((s32[]{:T(128)}, f32[128,25,64]{0,2,1:T(8,128)}, ...), condition=%wide.region_14.15_spmd.clone, body=%wide.region_13.14_spmd.clone.sunk | while | flops 639451136 | bytes 20651656 | solution.py:193
  749.6 29.6 %all_gather.54 = f32[1024,25]{0,1:T(8,128)S(1)} all-gather(f32[128,25]{0,1:T(8,128)S(1)} %bitcast.353), channel_id=1, replica_groups=mesh['ctx'=8,'fsdp'=4] {'ctx'}, dimensions={0}, use_global_device_ids=true | all-gather | bytes 115200 | tf_op jit(solution)/shard_map/all_gather | solution.py:200
  793.4 56.4 %all-gather.27.cloned.1.call-done = bf16[1024,1600]{0,1:T(8,128)(2,1)} async-done(((bf16[128,1600]{0,1:T(8,128)(2,1)}), bf16[1024,1600]{0,1:T(8,128)(2,1)}) %all-gather.27.cloned.1.call-update) | async-done | bytes 3276816 | tf_op jit(solution)/shard_map/all_gather | solution.py:196
  863.4 41.6 %while.51 = (s32[]{:T(128)}, f32[128,25,64]{0,2,1:T(8,128)}, f32[128,25,64]{0,2,1:T(8,128)}, bf16[2,512,25,64]{1,3,2,0:T(8,128)(2,1)S(1)}, s32[128]{0:T(128)S(1)...) while((s32[]{:T(128)}, f32[128,25,64]{0,2,1:T(8,128)}, ...), condition=%wide.region_16.17_spmd.clone, body=%wide.region_15.16_spmd.clone.sunk | while | flops 856129536 | bytes 31107220 | solution.py:225
  914.6 48.3 %all-to-all-done = bf16[128,8,600]{0,2,1:T(8,128)(2,1)S(1)} async-done(((bf16[128,8,600]{0,2,1:T(8,128)(2,1)}), bf16[128,8,600]{0,2,1:T(8,128)(2,1)S(1)}, u32[]{:S(2)}, u32[]{:S(2)}) %all-to-all-start) | async-done | bytes 1228832 | tf_op jit(solution)/shard_map/all_to_all | solution.py:44
  969.0 29.7 %all_to_all.76 = bf16[128,8,200]{0,2,1:T(8,128)(2,1)S(1)} all-to-all(bf16[128,8,200]{0,2,1:T(8,128)(2,1)S(1)} %bitcast.332), channel_id=1, replica_groups=mesh['ctx'=8,'fsdp'=4] {'ctx'}, dimensions={1} | all-to-all | bytes 819200 | tf_op jit(solution)/shard_map/all_to_all | solution.py:44
  998.7 120.4 %all-gather.35.cloned.1.call-done = bf16[1024,6400]{1,0:T(8,128)(2,1)} async-done(((bf16[128,6400]{1,0:T(8,128)(2,1)}), bf16[1024,6400]{1,0:T(8,128)(2,1)}) %all-gather.35.cloned.1.call-update) | async-done | bytes 13107216 | tf_op jit(solution)/shard_map/all_gather | solution.py:43
  1147.2 13.3 fusion.136
  1162.2 21.4 %reduce-scatter.11.cloned.1.call-done = bf16[400,800]{1,0:T(8,128)(2,1)} async-done(((bf16[1600,800]{1,0:T(8,128)(2,1)}), bf16[400,800]{1,0:T(8,128)(2,1)}) %reduce-scatter.11.cloned.1.call-update) | async-done | bytes 640016 | tf_op jit(solution)/shard_map/reduce_scatter | solution.py:37
  1185.9 31.0 %reduce-scatter.7.cloned.1.call-done = bf16[400,600]{1,0:T(8,128)(2,1)} async-done(((bf16[1600,600]{1,0:T(8,128)(2,1)}), bf16[400,600]{1,0:T(8,128)(2,1)}) %reduce-scatter.7.cloned.1.call-update) | async-done | bytes 480016 | tf_op jit(solution)/shard_map/reduce_scatter | solution.py:37
  1219.0 39.1 %reduce-scatter.13.cloned.1.call-done = bf16[1600,200]{1,0:T(8,128)(2,1)} async-done(((bf16[6400,200]{1,0:T(8,128)(2,1)}), bf16[1600,200]{1,0:T(8,128)(2,1)}) %reduce-scatter.13.cloned.1.call-update) | async-done | bytes 640016
  1260.8 133.7 %all-reduce.3.cloned.1.call-done = (f32[1600]{0:T(1024)}, f32[1600]{0:T(1024)}, f32[1600]{0:T(1024)}, f32[6400]{0:T(1024)}, f32[1600]{0:T(1024)}, /*index=5*/f32...) async-done(((f32[1600]{0:T(1024)}, f32[1600]{0:T(1024)}, f32[1600]{0:T(1024)}, f32[6400]{0:T(1024)}, f32[1600]{0:T(1024)}, /*index=5*/f32[1600]{0:T(1024)}, ...) | async-done | bytes 76816 | tf_op jit(solution)/shard_map/psum | solution.py:249
  (234 shorter events, 282.7 us)
Async XLA Ops:
  7.2 102.6 %all-gather.13.cloned.1.call-start = ((), (), s32[]{:S(2)}) async-start(), calls=%async_computation.8 | async-start | bytes 19456000 | tf_op jit(solution)/shard_map/all_gather | solution.py:27
  7.9 174.7 %all-gather.17.cloned.1.call-start = ((), (), s32[]{:S(2)}) async-start(), calls=%async_computation.10 | async-start | bytes 3686400 | tf_op jit(solution)/shard_map/all_gather | solution.py:99
  9.7 109.7 %copy-start.12 = (bf16[128,1600]{0,1:T(8,128)(2,1)}, bf16[128,1600]{0,1:T(8,128)(2,1)S(1)}, u32[]{:S(2)}) copy-start(bf16[128,1600]{0,1:T(8,128)(2,1)S(1)} %fusion.149) | copy-start | bytes 1228804
  9.8 110.5 %copy-start.22 = (f32[1600]{0:T(1024)S(1)}, f32[1600]{0:T(1024)}, u32[]{:S(2)}) copy-start(f32[1600]{0:T(1024)} %param.27) | copy-start | bytes 19204
  9.8 110.5 %copy-start.23 = (f32[1600]{0:T(1024)S(1)}, f32[1600]{0:T(1024)}, u32[]{:S(2)}) copy-start(f32[1600]{0:T(1024)} %param.28) | copy-start | bytes 19204
  120.2 127.5 %all-gather.15.cloned.1.call-start = ((), (), s32[]{:S(2)}) async-start(), calls=%async_computation.9 | async-start | bytes 3686400 | tf_op jit(solution)/shard_map/all_gather | solution.py:100
  121.7 170.8 %all-gather.19.cloned.1.call-start = ((), (), s32[]{:S(2)}) async-start(), calls=%async_computation.11 | async-start | bytes 6656000 | tf_op jit(solution)/shard_map/all_gather | solution.py:27
  122.3 298.1 %all-gather.21.cloned.1.call-start = ((), (), s32[]{:S(2)}) async-start(), calls=%async_computation.12 | async-start | bytes 25600000 | tf_op jit(solution)/shard_map/all_gather | solution.py:27
  122.9 432.3 %all-gather.23.cloned.1.call-start = ((), (), s32[]{:S(2)}) async-start(), calls=%async_computation.13 | async-start | bytes 26624000 | tf_op jit(solution)/shard_map/all_gather | solution.py:27
  123.4 512.6 %all-gather.25.cloned.1.call-start = ((), (), s32[]{:S(2)}) async-start(), calls=%async_computation.14 | async-start | bytes 3686400 | tf_op jit(solution)/shard_map/all_gather | solution.py:195
  124.2 596.8 %all-gather.31.cloned.1.call-start = ((), (), s32[]{:S(2)}) async-start(), calls=%async_computation.18 | async-start | bytes 3686400 | tf_op jit(solution)/shard_map/all_gather | solution.py:43
  292.4 127.9 %copy-start.18 = (f32[6400]{0:T(1024)S(1)}, f32[6400]{0:T(1024)}, u32[]{:S(2)}) copy-start(f32[6400]{0:T(1024)} %param.32) | copy-start | bytes 76804
  292.4 493.4 %all-gather.33.cloned.1.call-start = ((), (), s32[]{:S(2)}) async-start(), calls=%async_computation.20 | async-start | bytes 3686400 | tf_op jit(solution)/shard_map/all_gather | solution.py:43
  299.6 550.2 %all-gather.27.cloned.1.call-start = ((), (), s32[]{:S(2)}) async-start(), calls=%async_computation.15 | async-start | bytes 3686400 | tf_op jit(solution)/shard_map/all_gather | solution.py:196
  585.6 329.0 %all-gather.29.cloned.1.call-start = ((), (), s32[]{:S(2)}) async-start(), calls=%async_computation.16 | async-start | bytes 3686400 | tf_op jit(solution)/shard_map/all_gather | solution.py:43
  586.3 532.7 %all-gather.35.cloned.1.call-start = ((), (), s32[]{:S(2)}) async-start(), calls=%async_computation.22 | async-start | bytes 14745600 | tf_op jit(solution)/shard_map/all_gather | solution.py:43
  586.9 67.2 %all-to-all-start.1 = ((bf16[128,8,200]{0,2,1:T(8,128)(2,1)}), bf16[128,8,200]{0,2,1:T(8,128)(2,1)}, u32[]{:S(2)}, u32[]{:S(2)}) async-start(bf16[128,8,200]{0,2,1:T(8,128)(2,1)} %bitcast.347), calls=%async_computation.2 | async-start | bytes 819200 | tf_op jit(solution)/shard_map/all_to_all | solution.py:44
  654.1 127.9 %all-to-all-start.2 = ((bf16[128,8,800]{0,2,1:T(8,128)(2,1)}), bf16[128,8,800]{0,2,1:T(8,128)(2,1)}, u32[]{:S(2)}, u32[]{:S(2)}) async-start(bf16[128,8,800]{0,2,1:T(8,128)(2,1)} %bitcast.329), calls=%async_computation.4 | async-start | bytes 3276800 | tf_op jit(solution)/shard_map/all_to_all | solution.py:44
  662.5 498.1 %reduce-scatter.9.cloned.1.call-start = ((), (), s32[]{:S(2)}) async-start(), calls=%async_computation.19 | async-start | bytes 1024000 | tf_op jit(solution)/shard_map/reduce_scatter | solution.py:37
  724.9 458.7 %reduce-scatter.11.cloned.1.call-start = ((), (), s32[]{:S(2)}) async-start(), calls=%async_computation.21 | async-start | bytes 3584000 | tf_op jit(solution)/shard_map/reduce_scatter | solution.py:37
  908.8 54.1 %all-to-all-start = ((bf16[128,8,600]{0,2,1:T(8,128)(2,1)}), bf16[128,8,600]{0,2,1:T(8,128)(2,1)S(1)}, u32[]{:S(2)}, u32[]{:S(2)}) async-start(bf16[128,8,600]{0,2,1:T(8,128)(2,1)} %bitcast.15), calls=%async_computation | async-start | bytes 2457600 | tf_op jit(solution)/shard_map/all_to_all | solution.py:44
  914.6 302.4 %reduce-scatter.7.cloned.1.call-start = ((), (), s32[]{:S(2)}) async-start(), calls=%async_computation.17 | async-start | bytes 2560000 | tf_op jit(solution)/shard_map/reduce_scatter | solution.py:37
  968.9 289.2 %reduce-scatter.13.cloned.1.call-start = ((), (), s32[]{:S(2)}) async-start(), calls=%async_computation.23 | async-start | bytes 4096000
  1132.9 261.6 %all-reduce.3.cloned.1.call-start = ((), (), s32[]{:S(2)}) async-start(), calls=%async_computation.24 | async-start | bytes 188416 | tf_op jit(solution)/shard_map/psum | solution.py:249
  (30 other events, 230.2 us)
Sparse Core Ops, SparseCore 0:
  9.6 100.1 all-gather.12
  120.3 62.2 all-gather.16
  185.3 62.3 all-gather.14
  249.1 40.8 all-gather.18
  291.4 128.8 all-gather.20
  421.8 133.3 all-gather.22
  557.8 69.9 all-gather.24
  629.9 91.0 all-gather.30
  723.0 62.7 all-gather.32
  787.7 62.1 all-gather.26
  851.9 62.3 all-gather.28
  916.3 202.6 all-gather.34
  1121.6 23.4 reduce-scatter.8
  1147.5 36.1 reduce-scatter.10
  1186.0 30.8 reduce-scatter.6
  1219.4 38.7 reduce-scatter.12
  1265.6 128.8 all-reduce.2
where the time goes:
time: 1420 us; the launch traced here: 1410 us
  waiting for transfers between devices  970 us (68%)
  matrix products  189 us (13%)
  blocking collectives  102 us (7%)
  local copies, waits for them, and re-layouts  82.1 us (6%)
  other arithmetic  34.4 us (2%)
  starting transfers between devices  21.4 us (2%)
  between operations  14.8 us (1%)
    all_gather x4, waiting for transfers between devices, fetch(): return lax.all_gather(weight, 'fsdp', axis=0, tiled=True)  341 us
    all_gather x4, waiting for transfers between devices, column_grad(): whole_left = lax.all_gather(left, 'ctx', axis=0, tiled=True)  183 us
    psum x1, waiting for transfers between devices, body(): lax.psum((grad_query_bias, grad_value_bias, grad_out_bias, grad_expand_bi...  134 us
    all_gather x1, waiting for transfers between devices, body(): lax.all_gather(keys_own, 'ctx', axis=0, tiled=True)  57.6 us
    all_gather x1, waiting for transfers between devices, body(): lax.all_gather(grad_att_low, 'ctx', axis=0, tiled=True)  56.4 us
    all_gather x1, waiting for transfers between devices, body(): lax.all_gather(values_own, 'ctx', axis=0, tiled=True)  53.8 us
    reduce_scatter x3, waiting for transfers between devices, shard_rows(): lax.psum_scatter(local.astype(jnp.bfloat16), 'fsdp', scatter_dimension=0,...  52.4 us
    all_to_all x3, waiting for transfers between devices, column_grad(): lax.all_to_all(right, 'ctx', split_axis=1, concat_axis=0, tiled=True)  48.3 us
  transfers between devices with their start and end apart: 20, of which 14 were waited for; matrix products, arithmetic and copies ran while one was open for 20% of the time, Pallas kernels for 0%

commit v1 on v0

--- a/solution.py
+++ b/solution.py
@@ -2,6 +2,7 @@
 import jax.numpy as jnp
 from jax import lax
 from jax.sharding import PartitionSpec as P
+from jax.lax import all_to_all, axis_size
 
 HEADS = 25
 HEAD_DIM = 64
@@ -41,7 +42,9 @@
 
 def column_grad(left, right):
     whole_left = lax.all_gather(left, "ctx", axis=0, tiled=True)
-    right_columns = lax.all_to_all(right, "ctx", split_axis=1, concat_axis=0, tiled=True)
+    right_columns = jnp.concatenate(
+        all_to_all(jnp.stack(jnp.split(right, axis_size("ctx"), axis=1)), "ctx", 0, 0), axis=0
+    )
     local = lax.dot_general(
         whole_left, right_columns, (((0,), (0,)), ((), ())), preferred_element_type=jnp.float32
     )

time: 1420 us -> 1420 us (level)
  local copies, waits for them, and re-layouts: 82.1 us -> 105 us
    unnamed x83 -> x117, local copies, waits for them, and re-layouts: 38 us -> 58.1 us
    all_gather x4, waiting for transfers between devices: 183 us -> 166 us  [column_grad(): whole_left = lax.all_gather(left, 'ctx', axis=0, tiled=True)]
  transfers between devices with their start and end apart: 20 -> 20, of which waited for: 14 -> 15; matrix products, arithmetic and copies ran while one was open for 20% -> 21% of each run, Pallas kernels for 0% -> 0%
where the time goes in v1:
time: 1420 us
  waiting for transfers between devices  960 us (68%)
  matrix products  189 us (13%)
  local copies, waits for them, and re-layouts  105 us (7%)
  blocking collectives  94.5 us (7%)
  other arithmetic  32.3 us (2%)
  starting transfers between devices  19.1 us (1%)
  between operations  15 us (1%)
    all_gather x4, waiting for transfers between devices, fetch(): return lax.all_gather(weight, 'fsdp', axis=0, tiled=True)  341 us
    all_gather x4, waiting for transfers between devices, column_grad(): whole_left = lax.all_gather(left, 'ctx', axis=0, tiled=True)  166 us
    psum x1, waiting for transfers between devices, body(): lax.psum((grad_query_bias, grad_value_bias, grad_out_bias, grad_expand_bi...  134 us
    unnamed x117, local copies, waits for them, and re-layouts  58.1 us
    all_gather x1, waiting for transfers between devices, body(): lax.all_gather(keys_own, 'ctx', axis=0, tiled=True)  57.6 us
    all_gather x1, waiting for transfers between devices, body(): lax.all_gather(grad_att_low, 'ctx', axis=0, tiled=True)  56.5 us
    all_gather x1, waiting for transfers between devices, body(): lax.all_gather(values_own, 'ctx', axis=0, tiled=True)  53.8 us
    reduce_scatter x3, waiting for transfers between devices, shard_rows(): lax.psum_scatter(local.astype(jnp.bfloat16), 'fsdp', scatter_dimension=0,...  53.5 us
  transfers between devices with their start and end apart: 20, of which 15 were waited for; matrix products, arithmetic and copies ran while one was open for 21% of the time, Pallas kernels for 0%

profile of v1, /device:TPU:8, one launch (start us, length us, event | category | flops | bytes accessed | tf_op | source)
XLA Modules:
  0.0 1415.7 jit_solution(6711984197787299136)
XLA Ops:
  9.8 100.0 %all-gather.13.cloned.1.call-done = bf16[1600,4800]{1,0:T(8,128)(2,1)} async-done(((bf16[400,4800]{1,0:T(8,128)(2,1)}), bf16[1600,4800]{1,0:T(8,128)(2,1)}) %all-gather.13.cloned.1.call-update) | async-done | bytes 15360016 | tf_op jit(solution)/shard_map/all_gather | solution.py:28
  125.1 57.6 %all-gather.17.cloned.1.call-done = bf16[1024,1600]{0,1:T(8,128)(2,1)} async-done(((bf16[128,1600]{0,1:T(8,128)(2,1)}), bf16[1024,1600]{0,1:T(8,128)(2,1)}) %all-gather.17.cloned.1.call-update) | async-done | bytes 3276816 | tf_op jit(solution)/shard_map/all_gather | solution.py:102
  193.9 53.8 %all-gather.15.cloned.1.call-done = bf16[1024,1600]{0,1:T(8,128)(2,1)} async-done(((bf16[128,1600]{0,1:T(8,128)(2,1)}), bf16[1024,1600]{0,1:T(8,128)(2,1)}) %all-gather.15.cloned.1.call-update) | async-done | bytes 3276816 | tf_op jit(solution)/shard_map/all_gather | solution.py:103
  261.0 19.3 %while.48 = (s32[]{:T(128)}, f32[25,128]{1,0:T(8,128)S(1)}, f32[25,128]{1,0:T(8,128)S(1)}, s32[2,512]{1,0:T(2,128)S(1)}, s32[128]{0:T(128)S(1)}, /*index=5*/bf16...) while((s32[]{:T(128)}, f32[25,128]{1,0:T(8,128)S(1)}, ...), condition=%wide.region_5.6_spmd.clone, body=%wide.region_2.5_spmd.clone.sunk | while | flops 221265536 | bytes 15524976 | solution.py:121
  299.9 120.4 %all-gather.21.cloned.1.call-done = bf16[1600,6400]{1,0:T(8,128)(2,1)} async-done(((bf16[400,6400]{1,0:T(8,128)(2,1)}), bf16[1600,6400]{1,0:T(8,128)(2,1)}) %all-gather.21.cloned.1.call-update) | async-done | bytes 20480016 | tf_op jit(solution)/shard_map/all_gather | solution.py:28
  420.3 14.0 multiply_convert_fusion.6
  434.3 120.9 %all-gather.23.cloned.1.call-done = bf16[6400,1600]{1,0:T(8,128)(2,1)} async-done(((bf16[1600,1600]{1,0:T(8,128)(2,1)}), bf16[6400,1600]{1,0:T(8,128)(2,1)}) %all-gather.23.cloned.1.call-update) | async-done | bytes 20480016 | tf_op jit(solution)/shard_map/all_gather | solution.py:28
  555.2 12.7 convert_reduce_fusion
  567.9 12.8 multiply_reduce_fusion
  587.4 30.4 %all_gather.52 = f32[1024,25]{0,1:T(8,128)S(1)} all-gather(f32[128,25]{0,1:T(8,128)S(1)} %bitcast.486), channel_id=1, replica_groups=mesh['ctx'=8,'fsdp'=4] {'ctx'}, dimensions={0}, use_global_device_ids=true | all-gather | bytes 115200 | tf_op jit(solution)/shard_map/all_gather | solution.py:202
  671.4 24.5 %while.50 = (s32[]{:T(128)}, f32[128,25,64]{0,2,1:T(8,128)}, bf16[2,512,25,64]{1,3,2,0:T(8,128)(2,1)S(1)}, s32[2,512]{1,0:T(2,128)S(1)}, s32[128]{0:T(128)S(1)},...) while((s32[]{:T(128)}, f32[128,25,64]{0,2,1:T(8,128)}, ...), condition=%wide.region_14.15_spmd.clone, body=%wide.region_13.14_spmd.clone.sunk | while | flops 639451136 | bytes 20651656 | solution.py:196
  695.9 19.7 %all-gather.31.cloned.1.call-done = bf16[1024,1600]{0,1:T(8,128)(2,1)} async-done(((bf16[128,1600]{0,1:T(8,128)(2,1)}), bf16[1024,1600]{0,1:T(8,128)(2,1)}) %all-gather.31.cloned.1.call-update) | async-done | bytes 3276816 | tf_op jit(solution)/shard_map/all_gather | solution.py:44
  719.9 35.4 %all_gather.54 = f32[1024,25]{0,1:T(8,128)S(1)} all-gather(f32[128,25]{0,1:T(8,128)S(1)} %bitcast.485), channel_id=1, replica_groups=mesh['ctx'=8,'fsdp'=4] {'ctx'}, dimensions={0}, use_global_device_ids=true | all-gather | bytes 115200 | tf_op jit(solution)/shard_map/all_gather | solution.py:203
  757.4 27.0 %all-gather.33.cloned.1.call-done = bf16[1024,1600]{0,1:T(8,128)(2,1)} async-done(((bf16[128,1600]{0,1:T(8,128)(2,1)}), bf16[1024,1600]{0,1:T(8,128)(2,1)}) %all-gather.33.cloned.1.call-update) | async-done | bytes 3276816 | tf_op jit(solution)/shard_map/all_gather | solution.py:44
  792.1 56.5 %all-gather.27.cloned.1.call-done = bf16[1024,1600]{0,1:T(8,128)(2,1)} async-done(((bf16[128,1600]{0,1:T(8,128)(2,1)}), bf16[1024,1600]{0,1:T(8,128)(2,1)}) %all-gather.27.cloned.1.call-update) | async-done | bytes 3276816 | tf_op jit(solution)/shard_map/all_gather | solution.py:199
  862.1 41.7 %while.51 = (s32[]{:T(128)}, f32[128,25,64]{0,2,1:T(8,128)}, f32[128,25,64]{0,2,1:T(8,128)}, bf16[2,512,25,64]{1,3,2,0:T(8,128)(2,1)S(1)}, s32[128]{0:T(128)S(1)...) while((s32[]{:T(128)}, f32[128,25,64]{0,2,1:T(8,128)}, ...), condition=%wide.region_16.17_spmd.clone, body=%wide.region_15.16_spmd.clone.sunk | while | flops 856129536 | bytes 31107220 | solution.py:228
  916.4 50.2 %all-to-all-done = bf16[8,128,600]{1,2,0:T(8,128)(2,1)S(1)} async-done(((bf16[8,128,600]{1,2,0:T(8,128)(2,1)}), bf16[8,128,600]{1,2,0:T(8,128)(2,1)S(1)}, u32[]{:S(2)}, u32[]{:S(2)}) %all-to-all-start) | async-done | bytes 1228832 | tf_op jit(solution)/shard_map/all_to_all | solution.py:46
  972.8 28.7 %all_to_all.20 = bf16[8,128,200]{1,2,0:T(8,128)(2,1)S(1)} all-to-all(bf16[8,128,200]{1,2,0:T(8,128)(2,1)S(1)} %constant_dynamic-update-slice_fusion.8), channel_id=1, replica_groups=mesh['ctx'=8,'fsdp'=4] {'ctx'}, dimensions={0} | all-to-all | bytes 819200 | tf_op jit(solution)/shard_map/all_to_all | solution.py:46
  1001.5 119.4 %all-gather.35.cloned.1.call-done = bf16[1024,6400]{1,0:T(8,128)(2,1)} async-done(((bf16[128,6400]{1,0:T(8,128)(2,1)}), bf16[1024,6400]{1,0:T(8,128)(2,1)}) %all-gather.35.cloned.1.call-update) | async-done | bytes 13107216 | tf_op jit(solution)/shard_map/all_gather | solution.py:44
  1135.5 13.3 fusion.136
  1163.6 22.4 %reduce-scatter.11.cloned.1.call-done = bf16[400,800]{1,0:T(8,128)(2,1)} async-done(((bf16[1600,800]{1,0:T(8,128)(2,1)}), bf16[400,800]{1,0:T(8,128)(2,1)}) %reduce-scatter.11.cloned.1.call-update) | async-done | bytes 640016 | tf_op jit(solution)/shard_map/reduce_scatter | solution.py:38
  1188.3 31.0 %reduce-scatter.7.cloned.1.call-done = bf16[400,600]{1,0:T(8,128)(2,1)} async-done(((bf16[1600,600]{1,0:T(8,128)(2,1)}), bf16[400,600]{1,0:T(8,128)(2,1)}) %reduce-scatter.7.cloned.1.call-update) | async-done | bytes 480016 | tf_op jit(solution)/shard_map/reduce_scatter | solution.py:38
  1221.4 39.1 %reduce-scatter.13.cloned.1.call-done = bf16[1600,200]{1,0:T(8,128)(2,1)} async-done(((bf16[6400,200]{1,0:T(8,128)(2,1)}), bf16[1600,200]{1,0:T(8,128)(2,1)}) %reduce-scatter.13.cloned.1.call-update) | async-done | bytes 640016
  1263.2 133.8 %all-reduce.3.cloned.1.call-done = (f32[1600]{0:T(1024)}, f32[1600]{0:T(1024)}, f32[1600]{0:T(1024)}, f32[6400]{0:T(1024)}, f32[1600]{0:T(1024)}, /*index=5*/f32...) async-done(((f32[1600]{0:T(1024)}, f32[1600]{0:T(1024)}, f32[1600]{0:T(1024)}, f32[6400]{0:T(1024)}, f32[1600]{0:T(1024)}, /*index=5*/f32[1600]{0:T(1024)}, ...) | async-done | bytes 76816 | tf_op jit(solution)/shard_map/psum | solution.py:252
  (273 shorter events, 311.0 us)
Async XLA Ops:
  7.2 102.6 %all-gather.13.cloned.1.call-start = ((), (), s32[]{:S(2)}) async-start(), calls=%async_computation.8 | async-start | bytes 19456000 | tf_op jit(solution)/shard_map/all_gather | solution.py:28
  7.9 174.7 %all-gather.17.cloned.1.call-start = ((), (), s32[]{:S(2)}) async-start(), calls=%async_computation.10 | async-start | bytes 3686400 | tf_op jit(solution)/shard_map/all_gather | solution.py:102
  9.7 109.6 %copy-start.13 = (bf16[128,1600]{0,1:T(8,128)(2,1)}, bf16[128,1600]{0,1:T(8,128)(2,1)S(1)}, u32[]{:S(2)}) copy-start(bf16[128,1600]{0,1:T(8,128)(2,1)S(1)} %fusion.155) | copy-start | bytes 1228804
  9.8 110.5 %copy-start.26 = (f32[1600]{0:T(1024)S(1)}, f32[1600]{0:T(1024)}, u32[]{:S(2)}) copy-start(f32[1600]{0:T(1024)} %param.27) | copy-start | bytes 19204
  9.8 110.5 %copy-start.27 = (f32[1600]{0:T(1024)S(1)}, f32[1600]{0:T(1024)}, u32[]{:S(2)}) copy-start(f32[1600]{0:T(1024)} %param.28) | copy-start | bytes 19204
  120.2 127.5 %all-gather.15.cloned.1.call-start = ((), (), s32[]{:S(2)}) async-start(), calls=%async_computation.9 | async-start | bytes 3686400 | tf_op jit(solution)/shard_map/all_gather | solution.py:103
  121.7 171.0 %all-gather.19.cloned.1.call-start = ((), (), s32[]{:S(2)}) async-start(), calls=%async_computation.11 | async-start | bytes 6656000 | tf_op jit(solution)/shard_map/all_gather | solution.py:28
  122.3 298.1 %all-gather.21.cloned.1.call-start = ((), (), s32[]{:S(2)}) async-start(), calls=%async_computation.12 | async-start | bytes 25600000 | tf_op jit(solution)/shard_map/all_gather | solution.py:28
  122.9 432.3 %all-gather.23.cloned.1.call-start = ((), (), s32[]{:S(2)}) async-start(), calls=%async_computation.13 | async-start | bytes 26624000 | tf_op jit(solution)/shard_map/all_gather | solution.py:28
  123.5 498.7 %all-gather.25.cloned.1.call-start = ((), (), s32[]{:S(2)}) async-start(), calls=%async_computation.14 | async-start | bytes 3686400 | tf_op jit(solution)/shard_map/all_gather | solution.py:198
  124.2 591.4 %all-gather.31.cloned.1.call-start = ((), (), s32[]{:S(2)}) async-start(), calls=%async_computation.18 | async-start | bytes 3686400 | tf_op jit(solution)/shard_map/all_gather | solution.py:44
  292.4 128.0 %copy-start.22 = (f32[6400]{0:T(1024)S(1)}, f32[6400]{0:T(1024)}, u32[]{:S(2)}) copy-start(f32[6400]{0:T(1024)} %param.32) | copy-start | bytes 76804
  292.4 492.0 %all-gather.33.cloned.1.call-start = ((), (), s32[]{:S(2)}) async-start(), calls=%async_computation.20 | async-start | bytes 3686400 | tf_op jit(solution)/shard_map/all_gather | solution.py:44
  299.9 548.7 %all-gather.27.cloned.1.call-start = ((), (), s32[]{:S(2)}) async-start(), calls=%async_computation.15 | async-start | bytes 3686400 | tf_op jit(solution)/shard_map/all_gather | solution.py:199
  586.1 330.3 %all-gather.29.cloned.1.call-start = ((), (), s32[]{:S(2)}) async-start(), calls=%async_computation.16 | async-start | bytes 3686400 | tf_op jit(solution)/shard_map/all_gather | solution.py:44
  586.8 534.0 %all-gather.35.cloned.1.call-start = ((), (), s32[]{:S(2)}) async-start(), calls=%async_computation.22 | async-start | bytes 14745600 | tf_op jit(solution)/shard_map/all_gather | solution.py:44
  640.1 25.3 %all-to-all-start.1 = ((bf16[8,128,200]{1,2,0:T(8,128)(2,1)}), bf16[8,128,200]{1,2,0:T(8,128)(2,1)}, u32[]{:S(2)}, u32[]{:S(2)}) async-start(bf16[8,128,200]{1,2,0:T(8,128)(2,1)} %constant_dynamic-update-slice_fusion), calls=%async_computation.2 | async-start | bytes 819200 | tf_op jit(solution)/shard_map/all_to_all | solution.py:46
  665.4 92.0 %all-to-all-start.2 = ((bf16[8,128,800]{1,2,0:T(8,128)(2,1)}), bf16[8,128,800]{1,2,0:T(8,128)(2,1)}, u32[]{:S(2)}, u32[]{:S(2)}) async-start(bf16[8,128,800]{1,2,0:T(8,128)(2,1)} %copy.106), calls=%async_computation.4 | async-start | bytes 3276800 | tf_op jit(solution)/shard_map/all_to_all | solution.py:46
  671.4 477.4 %reduce-scatter.9.cloned.1.call-start = ((), (), s32[]{:S(2)}) async-start(), calls=%async_computation.19 | async-start | bytes 1024000 | tf_op jit(solution)/shard_map/reduce_scatter | solution.py:38
  719.5 466.5 %reduce-scatter.11.cloned.1.call-start = ((), (), s32[]{:S(2)}) async-start(), calls=%async_computation.21 | async-start | bytes 3584000 | tf_op jit(solution)/shard_map/reduce_scatter | solution.py:38
  910.6 56.0 %all-to-all-start = ((bf16[8,128,600]{1,2,0:T(8,128)(2,1)}), bf16[8,128,600]{1,2,0:T(8,128)(2,1)S(1)}, u32[]{:S(2)}, u32[]{:S(2)}) async-start(bf16[8,128,600]{1,2,0:T(8,128)(2,1)} %fusion.174), calls=%async_computation | async-start | bytes 2457600 | tf_op jit(solution)/shard_map/all_to_all | solution.py:46
  916.4 302.9 %reduce-scatter.7.cloned.1.call-start = ((), (), s32[]{:S(2)}) async-start(), calls=%async_computation.17 | async-start | bytes 2560000 | tf_op jit(solution)/shard_map/reduce_scatter | solution.py:38
  972.6 287.9 %reduce-scatter.13.cloned.1.call-start = ((), (), s32[]{:S(2)}) async-start(), calls=%async_computation.23 | async-start | bytes 4096000
  1134.8 262.2 %all-reduce.3.cloned.1.call-start = ((), (), s32[]{:S(2)}) async-start(), calls=%async_computation.24 | async-start | bytes 188416 | tf_op jit(solution)/shard_map/psum | solution.py:252
  (34 other events, 379.3 us)
Sparse Core Ops, SparseCore 0:
  9.6 100.1 all-gather.12
  120.3 62.2 all-gather.16
  185.3 62.3 all-gather.14
  249.1 40.8 all-gather.18
  291.4 128.8 all-gather.20
  421.8 133.3 all-gather.22
  557.8 64.2 all-gather.24
  624.1 91.3 all-gather.30
  717.6 66.7 all-gather.32
  786.3 62.2 all-gather.26
  850.6 62.3 all-gather.28
  915.1 205.7 all-gather.34
  1124.0 23.4 reduce-scatter.8
  1149.8 36.1 reduce-scatter.10
  1188.4 30.8 reduce-scatter.6
  1221.8 38.7 reduce-scatter.12
  1268.0 128.9 all-reduce.2
